TPU v7x, 32 devices: a whole 2x2x4 slice. The times are simulated.
32 devices in a mesh: member: 2 (over core), section: 4 (over y, x), atoms: 4 (over z).
Axes of the slice: x: 2, y: 2, z: 4, core: 2. Of those that a mesh axis runs over, the one named last changes fastest.
Arguments:
- positions: float32 [8, 3, 512], P(None, None, 'atoms'), may hold values from -8 to 8
- atom_types: int32 [8, 512], P(None, 'atoms'), may hold values from 0 to 127
- neighbors: int32 [8, 512, 128], P(None, 'atoms'), may hold values from 0 to 511
- nbr_mask: int32 [8, 512, 128], P(None, 'atoms'), may hold values 0 or 1
- type_table: bfloat16 [2, 128, 128], P('member'), may hold values from -6 to 6
- norm_gain: bfloat16 [2, 4, 128], P('member', 'section'), may hold values from 0.25 to 1.75
- proj_weight: bfloat16 [2, 4, 128, 384], P('member', 'section'), may hold values from -0.5 to 0.5
- out_weight: bfloat16 [2, 4, 128, 128], P('member', 'section'), may hold values from -0.5 to 0.5
- force_coef: bfloat16 [2, 4, 4], P('member', 'section'), may hold values from -48 to 48
Outputs:
- atom_dev: float32 [8, 512], P('section', 'atoms')
- max_dev: float32 [8], P('section')
- mean_force: float32 [8, 3, 512], P('section', None, 'atoms')
Inputs may be any that keep to these rules, and one draw needn't show every extreme that they name: `neighbors`: indices of atoms of the same frame, repeats and the atom itself allowed.
All inputs are finite; a program needn't handle non-finite values. No bound on the sum of `nbr_mask` on one device may be relied on, other than what follows from the above.
Results may differ from a plain program's by a relative error of at most 0.013.
Values may be sent and summed in bfloat16 or wider, within the bound.
No kernel may reach another device: no remote copies, remote signals or barrier semaphores. Data moves between devices by JAX's collectives and lax.ppermute only.
A program may use at most 64 MiB of HBM per device.

v0:
```python
import math
import jax
import jax.numpy as jnp
from jax import lax
from jax.sharding import PartitionSpec as P


def geometry(nbr, mask, pos_all, pos_own):
    total_atoms = pos_all.shape[1]
    hit = (nbr[:, :, None] == lax.iota(jnp.int32, total_atoms)[None, None, :]).astype(jnp.float32)
    counts = jnp.sum(hit * mask.astype(jnp.float32)[:, :, None], 1)
    delta = pos_all[:, None, :] - pos_own[:, :, None]
    switch = 1.0 / (1.0 + 0.125 * jnp.sum(delta * delta, 0))
    return (counts * switch, delta)


def block_dev(h_in, gain, proj, outw, coef, pair, delta, slots):
    width = h_in.shape[1]
    heads = coef.shape[0]
    head_dim = width // heads
    count = h_in.shape[0]
    hf = h_in.astype(jnp.float32)
    normed = (
        hf * lax.rsqrt(jnp.mean(hf * hf, -1, keepdims=True) + 1e-06) * gain.astype(jnp.float32)
    ).astype(jnp.bfloat16)
    query = jnp.dot(normed, proj[:, :width], preferred_element_type=jnp.float32).astype(
        jnp.bfloat16
    )
    keyval = jnp.dot(
        lax.all_gather(normed, "atoms", axis=0, tiled=True),
        proj[:, width:],
        preferred_element_type=jnp.float32,
    ).astype(jnp.bfloat16)
    total_atoms = keyval.shape[0]
    query3 = query.reshape(count, heads, head_dim)
    keys = keyval[:, :width].reshape(total_atoms, heads, head_dim)
    values = keyval[:, width:].reshape(total_atoms, heads, head_dim)
    scores = jnp.einsum(
        "ahd,jhd->haj", query3, keys, preferred_element_type=jnp.float32
    ) / math.sqrt(head_dim)
    weights = jax.nn.sigmoid(scores) * pair[None]
    message = jnp.einsum(
        "haj,jhd->ahd", weights.astype(jnp.bfloat16), values, preferred_element_type=jnp.float32
    )
    message = (message / slots).reshape(count, width).astype(jnp.bfloat16)
    h_out = (hf + jnp.dot(message, outw, preferred_element_type=jnp.float32)).astype(jnp.bfloat16)
    pair_coef = jnp.einsum("h,haj->aj", coef.astype(jnp.float32), weights)
    force = jnp.einsum("aj,caj->ca", pair_coef, delta) / slots
    return (h_out, force)


def embed(types_now, table):
    onehot = (types_now[:, None] == lax.iota(jnp.int32, table.shape[0])[None, :]).astype(
        jnp.bfloat16
    )
    return jnp.dot(onehot, table, preferred_element_type=jnp.float32).astype(jnp.bfloat16)


def shards(
    positions,
    atom_types,
    neighbors,
    nbr_mask,
    type_table,
    norm_gain,
    proj_weight,
    out_weight,
    force_coef,
):
    n_section = lax.axis_size("section")
    section_idx = lax.axis_index("section")
    frames = atom_types.shape[0]
    per_section = frames // n_section
    count = atom_types.shape[1]
    slots = neighbors.shape[2]
    table = type_table[0]
    pos_all = lax.all_gather(positions, "atoms", axis=2, tiled=True)
    gains, projs, outs, coefs = (
        lax.all_gather(norm_gain, "section", axis=1, tiled=True),
        lax.all_gather(proj_weight, "section", axis=1, tiled=True),
        lax.all_gather(out_weight, "section", axis=1, tiled=True),
        lax.all_gather(force_coef, "section", axis=1, tiled=True),
    )
    first = section_idx * per_section

    def whole_frame(local, own_forces):
        frame = first + local
        nbr = lax.dynamic_index_in_dim(neighbors, frame, 0, keepdims=False)
        mask = lax.dynamic_index_in_dim(nbr_mask, frame, 0, keepdims=False)
        pos_now = lax.dynamic_index_in_dim(pos_all, frame, 0, keepdims=False)
        pos_own = lax.dynamic_index_in_dim(positions, frame, 0, keepdims=False)
        pair, delta = geometry(nbr, mask, pos_now, pos_own)
        h_cur = embed(lax.dynamic_index_in_dim(atom_types, frame, 0, keepdims=False), table)
        total = jnp.zeros((3, count), jnp.float32)
        for blk in range(n_section):
            h_cur, term = block_dev(
                h_cur, gains[0, blk], projs[0, blk], outs[0, blk], coefs[0, blk], pair, delta, slots
            )
            total = total + term
        return lax.dynamic_update_index_in_dim(own_forces, total, local, 0)

    own = lax.fori_loop(
        0, per_section, whole_frame, jnp.zeros((per_section, 3, count), jnp.float32)
    )
    members = lax.axis_size("member")
    mean_force = lax.psum(own, "member") / members
    centered = own - mean_force
    spread = lax.psum(jnp.sum(centered * centered, 1), "member") / members
    atom_dev = jnp.sqrt(spread)
    max_dev = lax.pmax(jnp.max(atom_dev, -1), "atoms")
    return (atom_dev, max_dev, mean_force)


def solution(mesh):
    return jax.shard_map(
        shards,
        mesh=mesh,
        in_specs=(
            P(None, None, "atoms"),
            P(None, "atoms"),
            P(None, "atoms", None),
            P(None, "atoms", None),
            P("member", None, None),
            P("member", "section", None),
            P("member", "section", None, None),
            P("member", "section", None, None),
            P("member", "section", None),
        ),
        out_specs=(P("section", "atoms"), P("section"), P("section", None, "atoms")),
        check_vma=False,
    )
```

profile of v0, /device:TPU:0, one launch (start us, length us, event | category | flops | bytes accessed | tf_op | source)
XLA Modules:
  0.0 200.3 jit_solution(8612434693529792498)
XLA Ops:
  0.6 9.5 %all_gather.44 = bf16[1,4,128]{2,0,1:T(2,128)(2,1)S(1)} all-gather(bf16[1,1,128]{2,0,1:T(2,128)(2,1)} %bitcast.301), channel_id=1, replica_groups=mesh['member'=2,'section'=4,'atoms'=4] {'section'}, dimensions={1}, use_global_device_ids=true | all-gather | bytes 1280 | tf_op jit(solution)/shard_map/all_gather | solution.py:79
  10.2 7.8 %all_gather.46 = bf16[1,4,4]{2,0,1:T(2,128)(2,1)S(1)} all-gather(bf16[1,1,4]{2,0,1:T(2,128)(2,1)} %bitcast.302), channel_id=1, replica_groups=mesh['member'=2,'section'=4,'atoms'=4] {'section'}, dimensions={1}, use_global_device_ids=true | all-gather | bytes 40 | tf_op jit(solution)/shard_map/all_gather | solution.py:82
  18.0 0.7 copy.31
  18.7 12.2 %all_gather.43 = f32[8,3,512]{2,1,0:T(4,128)S(1)} all-gather(f32[8,3,128]{2,1,0:T(4,128)S(1)} %copy.31), channel_id=1, replica_groups=mesh['member'=2,'section'=4,'atoms'=4] {'atoms'}, dimensions={2}, use_global_device_ids=true | all-gather | bytes 61440 | tf_op jit(solution)/shard_map/all_gather | solution.py:77
  30.9 7.7 %all_gather.47 = bf16[1,4,128,128]{3,2,0,1:T(8,128)(2,1)S(1)} all-gather(bf16[1,1,128,128]{3,2,0,1:T(8,128)(2,1)} %bitcast.300), channel_id=1, replica_groups=mesh['member'=2,'section'=4,'atoms'=4] {'section'}, dimensions={1}, use_global_device_ids=true | all-gather | bytes 163840 | tf_op jit(solution)/shard_map/all_gather | solution.py:81
  38.6 9.3 %all_gather.45 = bf16[1,4,128,384]{3,2,0,1:T(8,128)(2,1)S(1)} all-gather(bf16[1,1,128,384]{3,2,0,1:T(8,128)(2,1)} %bitcast.299), channel_id=1, replica_groups=mesh['member'=2,'section'=4,'atoms'=4] {'section'}, dimensions={1}, use_global_device_ids=true | all-gather | bytes 491520 | tf_op jit(solution)/shard_map/all_gather | solution.py:80
  47.9 137.4 %while.13 = (s32[]{:T(128)}, f32[2,3,128]{2,0,1:T(2,128)S(1)}, s32[]{:T(128)}, f32[8,3,512]{2,1,0:T(4,128)S(1)}, f32[8,3,128]{2,1,0:T(4,128)S(1)}, /*index=5*/s3...) while((s32[]{:T(128)}, f32[2,3,128]{2,0,1:T(2,128)S(1)}, ...), condition=%wide.region_7.8_spmd, body=%wide.region_0.7_spmd.sunk | while | flops 322554368 | bytes 20396256 | solution.py:102
  47.9 0.7 fusion.231
  49.0 0.9 convert_bitcast_fusion.2
  49.9 6.0 %select_reduce_fusion.2 = f32[128,512]{1,0:T(8,128)S(1)} fusion(f32[128,128]{1,0:T(8,128)S(1)} %get-tuple-element.420, s32[128,128]{1,0:T(8,128)S(1)} %get-tuple-element.421), kind=kLoop, calls=%fused_computation.clone.1 | loop fusion | flops 25100288 | bytes 393216 | tf_op jit(solution)/shard_map/while/body/eval_jaxpr/reduce_sum | solution.py:11
  55.8 12.3 %all_gather.52 = bf16[512,128]{0,1:T(8,128)(2,1)S(1)} all-gather(bf16[128,128]{0,1:T(8,128)(2,1)S(1)} %multiply_convert_fusion.8), channel_id=1, replica_groups=mesh['member'=2,'section'=4,'atoms'=4] {'atoms'}, dimensions={0}, use_global_device_ids=true | all-gather | bytes 163840 | tf_op jit(solution)/shard_map/while/body/eval_jaxpr/all_gather | solution.py:30
  69.7 0.5 fusion.249
  70.3 0.6 fusion.250
  71.6 12.3 %all_gather.53 = bf16[512,128]{0,1:T(8,128)(2,1)S(1)} all-gather(bf16[128,128]{0,1:T(8,128)(2,1)S(1)} %multiply_convert_fusion.9), channel_id=1, replica_groups=mesh['member'=2,'section'=4,'atoms'=4] {'atoms'}, dimensions={0}, use_global_device_ids=true | all-gather | bytes 163840 | tf_op jit(solution)/shard_map/while/body/eval_jaxpr/all_gather | solution.py:30
  84.1 0.5 fusion.236
  84.9 0.5 fusion.247
  85.5 0.6 fusion.248
  86.8 12.3 %all_gather.54 = bf16[512,128]{0,1:T(8,128)(2,1)S(1)} all-gather(bf16[128,128]{0,1:T(8,128)(2,1)S(1)} %multiply_convert_fusion.10), channel_id=1, replica_groups=mesh['member'=2,'section'=4,'atoms'=4] {'atoms'}, dimensions={0}, use_global_device_ids=true | all-gather | bytes 163840 | tf_op jit(solution)/shard_map/while/body/eval_jaxpr/all_gather | solution.py:30
  99.3 0.5 fusion.239
  100.1 0.5 fusion.245
  100.6 0.6 fusion.246
  101.9 12.5 %all_gather.55 = bf16[512,128]{0,1:T(8,128)(2,1)S(1)} all-gather(bf16[128,128]{0,1:T(8,128)(2,1)S(1)} %multiply_convert_fusion.11), channel_id=1, replica_groups=mesh['member'=2,'section'=4,'atoms'=4] {'atoms'}, dimensions={0}, use_global_device_ids=true | all-gather | bytes 163840 | tf_op jit(solution)/shard_map/while/body/eval_jaxpr/all_gather | solution.py:30
  114.7 0.5 fusion.242
  115.2 0.5 fusion.243
  115.7 0.6 fusion.244
  116.5 0.7 fusion.231
  117.6 0.9 convert_bitcast_fusion.2
  118.5 6.0 %select_reduce_fusion.2 = f32[128,512]{1,0:T(8,128)S(1)} fusion(f32[128,128]{1,0:T(8,128)S(1)} %get-tuple-element.420, s32[128,128]{1,0:T(8,128)S(1)} %get-tuple-element.421), kind=kLoop, calls=%fused_computation.clone.1 | loop fusion | flops 25100288 | bytes 393216 | tf_op jit(solution)/shard_map/while/body/eval_jaxpr/reduce_sum | solution.py:11
  124.5 12.5 %all_gather.52 = bf16[512,128]{0,1:T(8,128)(2,1)S(1)} all-gather(bf16[128,128]{0,1:T(8,128)(2,1)S(1)} %multiply_convert_fusion.8), channel_id=1, replica_groups=mesh['member'=2,'section'=4,'atoms'=4] {'atoms'}, dimensions={0}, use_global_device_ids=true | all-gather | bytes 163840 | tf_op jit(solution)/shard_map/while/body/eval_jaxpr/all_gather | solution.py:30
  137.9 0.5 fusion.233
  138.7 0.5 fusion.249
  139.2 0.6 fusion.250
  140.5 12.4 %all_gather.53 = bf16[512,128]{0,1:T(8,128)(2,1)S(1)} all-gather(bf16[128,128]{0,1:T(8,128)(2,1)S(1)} %multiply_convert_fusion.9), channel_id=1, replica_groups=mesh['member'=2,'section'=4,'atoms'=4] {'atoms'}, dimensions={0}, use_global_device_ids=true | all-gather | bytes 163840 | tf_op jit(solution)/shard_map/while/body/eval_jaxpr/all_gather | solution.py:30
  153.2 0.5 fusion.236
  153.9 0.5 fusion.247
  154.5 0.6 fusion.248
  155.8 12.3 %all_gather.54 = bf16[512,128]{0,1:T(8,128)(2,1)S(1)} all-gather(bf16[128,128]{0,1:T(8,128)(2,1)S(1)} %multiply_convert_fusion.10), channel_id=1, replica_groups=mesh['member'=2,'section'=4,'atoms'=4] {'atoms'}, dimensions={0}, use_global_device_ids=true | all-gather | bytes 163840 | tf_op jit(solution)/shard_map/while/body/eval_jaxpr/all_gather | solution.py:30
  168.3 0.5 fusion.239
  169.1 0.5 fusion.245
  169.6 0.6 fusion.246
  170.9 12.3 %all_gather.55 = bf16[512,128]{0,1:T(8,128)(2,1)S(1)} all-gather(bf16[128,128]{0,1:T(8,128)(2,1)S(1)} %multiply_convert_fusion.11), channel_id=1, replica_groups=mesh['member'=2,'section'=4,'atoms'=4] {'atoms'}, dimensions={0}, use_global_device_ids=true | all-gather | bytes 163840 | tf_op jit(solution)/shard_map/while/body/eval_jaxpr/all_gather | solution.py:30
  184.0 0.5 fusion.243
  184.5 0.6 fusion.244
  185.3 2.5 %psum.14 = f32[2,3,128]{2,0,1:T(2,128)S(1)} all-reduce(f32[2,3,128]{2,0,1:T(2,128)S(1)} %get-tuple-element.217), channel_id=1, replica_groups=mesh['member'=2,'section'=4,'atoms'=4] {'member'}, use_global_device_ids=true, to_apply=%region_8.9 | all-reduce | flops 768 | bytes 6144 | tf_op jit(solution)/shard_map/psum | solution.py:106
  187.8 0.6 multiply_reduce_fusion.5
  188.3 2.4 %psum.15 = f32[2,128]{1,0:T(2,128)S(1)} all-reduce(f32[2,128]{1,0:T(2,128)S(1)} %get-tuple-element.285), channel_id=1, replica_groups=mesh['member'=2,'section'=4,'atoms'=4] {'member'}, use_global_device_ids=true, to_apply=%region_10.11 | all-reduce | flops 256 | bytes 2048 | tf_op jit(solution)/shard_map/psum | solution.py:108
  190.8 0.7 fusion.80
  191.5 8.9 %pmax.7 = f32[2]{0:T(128)} all-reduce(f32[2]{0:T(128)S(1)} %get-tuple-element.283), channel_id=1, replica_groups=mesh['member'=2,'section'=4,'atoms'=4] {'atoms'}, use_global_device_ids=true, to_apply=%region_12.13 | all-reduce | flops 2 | bytes 16 | tf_op jit(solution)/shard_map/pmax | solution.py:110
  (97 shorter events, 10.9 us)
Async XLA Ops:
  0.6 47.2 %copy-start = (bf16[1,128,128]{2,1,0:T(8,128)(2,1)S(1)}, bf16[1,128,128]{2,1,0:T(8,128)(2,1)}, u32[]{:S(2)}) copy-start(bf16[1,128,128]{2,1,0:T(8,128)(2,1)} %param.15) | copy-start | bytes 98308
where the time goes:
time: 201 us; the launch traced here: 200 us
  blocking collectives  159 us (79%)
  matrix products  20.5 us (10%)
  other arithmetic  16.4 us (8%)
  local copies, waits for them, and re-layouts  3.21 us (2%)
    all_gather x8, blocking collectives, block_dev(): lax.all_gather(normed, 'atoms', axis=0, tiled=True)  98.7 us
    all_gather x1, blocking collectives, shards(): pos_all = lax.all_gather(positions, 'atoms', axis=2, tiled=True)  12.2 us
    reduce_sum x2, other arithmetic, geometry(): counts = jnp.sum(hit * mask.astype(jnp.float32)[:, :, None], 1)  11.9 us
    all_gather x1, blocking collectives, shards(): lax.all_gather(norm_gain, 'section', axis=1, tiled=True)  9.53 us
    all_gather x1, blocking collectives, shards(): lax.all_gather(proj_weight, 'section', axis=1, tiled=True)  9.27 us
    pmax x1, blocking collectives, shards(): max_dev = lax.pmax(jnp.max(atom_dev, -1), 'atoms')  8.87 us
    all_gather x1, blocking collectives, shards(): lax.all_gather(force_coef, 'section', axis=1, tiled=True)  7.81 us
    all_gather x1, blocking collectives, shards(): lax.all_gather(out_weight, 'section', axis=1, tiled=True)  7.68 us

commit v1 on v0

--- a/solution.py
+++ b/solution.py
@@ -3,6 +3,13 @@
 import jax.numpy as jnp
 from jax import lax
 from jax.sharding import PartitionSpec as P
+
+
+def swapped_in(value, mesh_axis, along):
+    size = lax.axis_size(mesh_axis)
+    blocks = jnp.stack([value for _ in range(size)])
+    blocks = lax.all_to_all(blocks, mesh_axis, split_axis=0, concat_axis=0)
+    return jnp.concatenate(blocks, axis=along)
 
 
 def geometry(nbr, mask, pos_all, pos_own):
@@ -27,9 +34,7 @@
         jnp.bfloat16
     )
     keyval = jnp.dot(
-        lax.all_gather(normed, "atoms", axis=0, tiled=True),
-        proj[:, width:],
-        preferred_element_type=jnp.float32,
+        swapped_in(normed, "atoms", 0), proj[:, width:], preferred_element_type=jnp.float32
     ).astype(jnp.bfloat16)
     total_atoms = keyval.shape[0]
     query3 = query.reshape(count, heads, head_dim)

time: 201 us -> 176 us (0.88)
  blocking collectives: 159 us -> 61.7 us
  waiting for transfers between devices: 0 us -> 35 us
  starting transfers between devices: 0 us -> 30.2 us
  local copies, waits for them, and re-layouts: 3.21 us -> 9.51 us
    all_gather x8 -> x0, blocking collectives: 98.7 us -> none  [block_dev(): lax.all_gather(normed, 'atoms', axis=0, tiled=True)]
    all_to_all x0 -> x8, waiting for transfers between devices: none -> 35 us  [swapped_in(): blocks = lax.all_to_all(blocks, mesh_axis, split_axis=0, concat_axis=0)]
    all_to_all x0 -> x8, starting transfers between devices: none -> 30.2 us  [swapped_in(): blocks = lax.all_to_all(blocks, mesh_axis, split_axis=0, concat_axis=0)]
    another operation x0 -> x8, local copies, waits for them, and re-layouts: none -> 5.33 us  [swapped_in(): blocks = jnp.stack([value for _ in range(size)])]
  transfers between devices with their start and end apart: 0 -> 8, of which waited for: 0 -> 6; matrix products, arithmetic and copies ran while one was open for 0% -> 9% of each run, Pallas kernels for 0% -> 0%
where the time goes in v1:
time: 176 us; the launch traced here: 175 us
  blocking collectives  61.7 us (35%)
  waiting for transfers between devices  35 us (20%)
  starting transfers between devices  30.2 us (17%)
  matrix products  20.3 us (12%)
  other arithmetic  16.4 us (9%)
  local copies, waits for them, and re-layouts  9.51 us (5%)
    all_to_all x8, waiting for transfers between devices, swapped_in(): blocks = lax.all_to_all(blocks, mesh_axis, split_axis=0, concat_axis=0)  35 us
    all_to_all x8, starting transfers between devices, swapped_in(): blocks = lax.all_to_all(blocks, mesh_axis, split_axis=0, concat_axis=0)  30.2 us
    all_gather x1, blocking collectives, shards(): pos_all = lax.all_gather(positions, 'atoms', axis=2, tiled=True)  12.2 us
    reduce_sum x2, other arithmetic, geometry(): counts = jnp.sum(hit * mask.astype(jnp.float32)[:, :, None], 1)  11.9 us
    pmax x1, blocking collectives, shards(): max_dev = lax.pmax(jnp.max(atom_dev, -1), 'atoms')  10.3 us
    all_gather x1, blocking collectives, shards(): lax.all_gather(norm_gain, 'section', axis=1, tiled=True)  9.53 us
    all_gather x1, blocking collectives, shards(): lax.all_gather(proj_weight, 'section', axis=1, tiled=True)  9.27 us
    all_gather x1, blocking collectives, shards(): lax.all_gather(force_coef, 'section', axis=1, tiled=True)  7.81 us
  transfers between devices with their start and end apart: 8, of which 6 were waited for; matrix products, arithmetic and copies ran while one was open for 9% of the time, Pallas kernels for 0%

profile of v1, /device:TPU:0, one launch (start us, length us, event | category | flops | bytes accessed | tf_op | source)
XLA Modules:
  0.0 174.6 jit_solution(10347777580018066206)
XLA Ops:
  0.6 9.5 %all_gather.16 = bf16[1,4,128]{2,0,1:T(2,128)(2,1)S(1)} all-gather(bf16[1,1,128]{2,0,1:T(2,128)(2,1)} %bitcast.317), channel_id=1, replica_groups=mesh['member'=2,'section'=4,'atoms'=4] {'section'}, dimensions={1}, use_global_device_ids=true | all-gather | bytes 1280 | tf_op jit(solution)/shard_map/all_gather | solution.py:84
  10.2 7.8 %all_gather.18 = bf16[1,4,4]{2,0,1:T(2,128)(2,1)S(1)} all-gather(bf16[1,1,4]{2,0,1:T(2,128)(2,1)} %bitcast.318), channel_id=1, replica_groups=mesh['member'=2,'section'=4,'atoms'=4] {'section'}, dimensions={1}, use_global_device_ids=true | all-gather | bytes 40 | tf_op jit(solution)/shard_map/all_gather | solution.py:87
  18.0 0.7 copy.47
  18.7 12.2 %all_gather.15 = f32[8,3,512]{2,1,0:T(4,128)S(1)} all-gather(f32[8,3,128]{2,1,0:T(4,128)S(1)} %copy.47), channel_id=1, replica_groups=mesh['member'=2,'section'=4,'atoms'=4] {'atoms'}, dimensions={2}, use_global_device_ids=true | all-gather | bytes 61440 | tf_op jit(solution)/shard_map/all_gather | solution.py:82
  30.9 7.7 %all_gather.19 = bf16[1,4,128,128]{3,2,0,1:T(8,128)(2,1)S(1)} all-gather(bf16[1,1,128,128]{3,2,0,1:T(8,128)(2,1)} %bitcast.316), channel_id=1, replica_groups=mesh['member'=2,'section'=4,'atoms'=4] {'section'}, dimensions={1}, use_global_device_ids=true | all-gather | bytes 163840 | tf_op jit(solution)/shard_map/all_gather | solution.py:86
  38.6 9.3 %all_gather.17 = bf16[1,4,128,384]{3,2,0,1:T(8,128)(2,1)S(1)} all-gather(bf16[1,1,128,384]{3,2,0,1:T(8,128)(2,1)} %bitcast.315), channel_id=1, replica_groups=mesh['member'=2,'section'=4,'atoms'=4] {'section'}, dimensions={1}, use_global_device_ids=true | all-gather | bytes 491520 | tf_op jit(solution)/shard_map/all_gather | solution.py:85
  47.9 110.2 %while.13 = (s32[]{:T(128)}, f32[2,3,128]{2,0,1:T(2,128)S(1)}, s32[]{:T(128)}, f32[8,3,512]{2,1,0:T(4,128)S(1)}, f32[8,3,128]{2,1,0:T(4,128)S(1)}, /*index=5*/s3...) while((s32[]{:T(128)}, f32[2,3,128]{2,0,1:T(2,128)S(1)}, ...), condition=%wide.region_7.8_spmd, body=%wide.region_0.7_spmd.sunk | while | flops 322554368 | bytes 22231392 | solution.py:107
  47.9 0.7 fusion.231
  49.1 0.7 stack.48
  49.8 3.4 %all-to-all-start = ((bf16[4,128,128]{2,1,0:T(8,128)(2,1)}), bf16[4,128,128]{2,1,0:T(8,128)(2,1)S(1)}, u32[]{:S(2)}, u32[]{:S(2)}) async-start(bf16[4,128,128]{2,1,0:T(8,128)(2,1)} %stack.48), calls=%async_computation | async-start | bytes 262144 | tf_op jit(solution)/shard_map/while/body/eval_jaxpr/all_to_all | solution.py:11
  53.5 0.9 convert_bitcast_fusion.2
  54.4 6.0 %select_reduce_fusion.2 = f32[128,512]{1,0:T(8,128)S(1)} fusion(f32[128,128]{1,0:T(8,128)S(1)} %get-tuple-element.420, s32[128,128]{1,0:T(8,128)S(1)} %get-tuple-element.421), kind=kLoop, calls=%fused_computation.clone.1 | loop fusion | flops 25100288 | bytes 393216 | tf_op jit(solution)/shard_map/while/body/eval_jaxpr/reduce_sum | solution.py:18
  62.3 0.6 fusion.250
  63.5 0.7 stack.49
  64.1 5.1 %all-to-all-start.1 = ((bf16[4,128,128]{2,1,0:T(8,128)(2,1)}), bf16[4,128,128]{2,1,0:T(8,128)(2,1)S(1)}, u32[]{:S(2)}, u32[]{:S(2)}) async-start(bf16[4,128,128]{2,1,0:T(8,128)(2,1)} %stack.49), calls=%async_computation.1 | async-start | bytes 262144 | tf_op jit(solution)/shard_map/while/body/eval_jaxpr/all_to_all | solution.py:11
  69.4 6.4 %all-to-all-done.1 = bf16[4,128,128]{2,1,0:T(8,128)(2,1)S(1)} async-done(((bf16[4,128,128]{2,1,0:T(8,128)(2,1)}), bf16[4,128,128]{2,1,0:T(8,128)(2,1)S(1)}, u32[]{:S(2)}, u32[]{:S(2)}) %all-to-all-start.1) | async-done | bytes 131104 | tf_op jit(solution)/shard_map/while/body/eval_jaxpr/all_to_all | solution.py:11
  77.4 0.6 fusion.248
  78.6 0.7 stack.50
  79.3 3.4 %all-to-all-start.2 = ((bf16[4,128,128]{2,1,0:T(8,128)(2,1)}), bf16[4,128,128]{2,1,0:T(8,128)(2,1)S(1)}, u32[]{:S(2)}, u32[]{:S(2)}) async-start(bf16[4,128,128]{2,1,0:T(8,128)(2,1)} %stack.50), calls=%async_computation.2 | async-start | bytes 262144 | tf_op jit(solution)/shard_map/while/body/eval_jaxpr/all_to_all | solution.py:11
  82.9 5.9 %all-to-all-done.2 = bf16[4,128,128]{2,1,0:T(8,128)(2,1)S(1)} async-done(((bf16[4,128,128]{2,1,0:T(8,128)(2,1)}), bf16[4,128,128]{2,1,0:T(8,128)(2,1)S(1)}, u32[]{:S(2)}, u32[]{:S(2)}) %all-to-all-start.2) | async-done | bytes 131104 | tf_op jit(solution)/shard_map/while/body/eval_jaxpr/all_to_all | solution.py:11
  90.3 0.6 fusion.246
  91.5 0.7 stack.51
  92.2 3.3 %all-to-all-start.3 = ((bf16[4,128,128]{2,1,0:T(8,128)(2,1)}), bf16[4,128,128]{2,1,0:T(8,128)(2,1)S(1)}, u32[]{:S(2)}, u32[]{:S(2)}) async-start(bf16[4,128,128]{2,1,0:T(8,128)(2,1)} %stack.51), calls=%async_computation.3 | async-start | bytes 262144 | tf_op jit(solution)/shard_map/while/body/eval_jaxpr/all_to_all | solution.py:11
  95.7 5.7 %all-to-all-done.3 = bf16[4,128,128]{2,1,0:T(8,128)(2,1)S(1)} async-done(((bf16[4,128,128]{2,1,0:T(8,128)(2,1)}), bf16[4,128,128]{2,1,0:T(8,128)(2,1)S(1)}, u32[]{:S(2)}, u32[]{:S(2)}) %all-to-all-start.3) | async-done | bytes 131104 | tf_op jit(solution)/shard_map/while/body/eval_jaxpr/all_to_all | solution.py:11
  102.7 0.6 fusion.244
  103.5 0.7 fusion.231
  104.7 0.7 stack.48
  105.4 3.3 %all-to-all-start = ((bf16[4,128,128]{2,1,0:T(8,128)(2,1)}), bf16[4,128,128]{2,1,0:T(8,128)(2,1)S(1)}, u32[]{:S(2)}, u32[]{:S(2)}) async-start(bf16[4,128,128]{2,1,0:T(8,128)(2,1)} %stack.48), calls=%async_computation | async-start | bytes 262144 | tf_op jit(solution)/shard_map/while/body/eval_jaxpr/all_to_all | solution.py:11
  109.1 0.9 convert_bitcast_fusion.2
  110.0 6.0 %select_reduce_fusion.2 = f32[128,512]{1,0:T(8,128)S(1)} fusion(f32[128,128]{1,0:T(8,128)S(1)} %get-tuple-element.420, s32[128,128]{1,0:T(8,128)S(1)} %get-tuple-element.421), kind=kLoop, calls=%fused_computation.clone.1 | loop fusion | flops 25100288 | bytes 393216 | tf_op jit(solution)/shard_map/while/body/eval_jaxpr/reduce_sum | solution.py:18
  117.8 0.6 fusion.250
  119.0 0.7 stack.49
  119.7 5.0 %all-to-all-start.1 = ((bf16[4,128,128]{2,1,0:T(8,128)(2,1)}), bf16[4,128,128]{2,1,0:T(8,128)(2,1)S(1)}, u32[]{:S(2)}, u32[]{:S(2)}) async-start(bf16[4,128,128]{2,1,0:T(8,128)(2,1)} %stack.49), calls=%async_computation.1 | async-start | bytes 262144 | tf_op jit(solution)/shard_map/while/body/eval_jaxpr/all_to_all | solution.py:11
  124.9 5.7 %all-to-all-done.1 = bf16[4,128,128]{2,1,0:T(8,128)(2,1)S(1)} async-done(((bf16[4,128,128]{2,1,0:T(8,128)(2,1)}), bf16[4,128,128]{2,1,0:T(8,128)(2,1)S(1)}, u32[]{:S(2)}, u32[]{:S(2)}) %all-to-all-start.1) | async-done | bytes 131104 | tf_op jit(solution)/shard_map/while/body/eval_jaxpr/all_to_all | solution.py:11
  132.2 0.6 fusion.248
  133.4 0.7 stack.50
  134.1 3.3 %all-to-all-start.2 = ((bf16[4,128,128]{2,1,0:T(8,128)(2,1)}), bf16[4,128,128]{2,1,0:T(8,128)(2,1)S(1)}, u32[]{:S(2)}, u32[]{:S(2)}) async-start(bf16[4,128,128]{2,1,0:T(8,128)(2,1)} %stack.50), calls=%async_computation.2 | async-start | bytes 262144 | tf_op jit(solution)/shard_map/while/body/eval_jaxpr/all_to_all | solution.py:11
  137.6 5.7 %all-to-all-done.2 = bf16[4,128,128]{2,1,0:T(8,128)(2,1)S(1)} async-done(((bf16[4,128,128]{2,1,0:T(8,128)(2,1)}), bf16[4,128,128]{2,1,0:T(8,128)(2,1)S(1)}, u32[]{:S(2)}, u32[]{:S(2)}) %all-to-all-start.2) | async-done | bytes 131104 | tf_op jit(solution)/shard_map/while/body/eval_jaxpr/all_to_all | solution.py:11
  144.9 0.6 fusion.246
  146.1 0.7 stack.51
  146.8 3.3 %all-to-all-start.3 = ((bf16[4,128,128]{2,1,0:T(8,128)(2,1)}), bf16[4,128,128]{2,1,0:T(8,128)(2,1)S(1)}, u32[]{:S(2)}, u32[]{:S(2)}) async-start(bf16[4,128,128]{2,1,0:T(8,128)(2,1)} %stack.51), calls=%async_computation.3 | async-start | bytes 262144 | tf_op jit(solution)/shard_map/while/body/eval_jaxpr/all_to_all | solution.py:11
  150.3 5.7 %all-to-all-done.3 = bf16[4,128,128]{2,1,0:T(8,128)(2,1)S(1)} async-done(((bf16[4,128,128]{2,1,0:T(8,128)(2,1)}), bf16[4,128,128]{2,1,0:T(8,128)(2,1)S(1)}, u32[]{:S(2)}, u32[]{:S(2)}) %all-to-all-start.3) | async-done | bytes 131104 | tf_op jit(solution)/shard_map/while/body/eval_jaxpr/all_to_all | solution.py:11
  157.3 0.6 fusion.244
  158.1 2.5 %psum.14 = f32[2,3,128]{2,0,1:T(2,128)S(1)} all-reduce(f32[2,3,128]{2,0,1:T(2,128)S(1)} %get-tuple-element.217), channel_id=1, replica_groups=mesh['member'=2,'section'=4,'atoms'=4] {'member'}, use_global_device_ids=true, to_apply=%region_8.9 | all-reduce | flops 768 | bytes 6144 | tf_op jit(solution)/shard_map/psum | solution.py:111
  160.6 0.6 multiply_reduce_fusion.5
  161.2 2.4 %psum.15 = f32[2,128]{1,0:T(2,128)S(1)} all-reduce(f32[2,128]{1,0:T(2,128)S(1)} %get-tuple-element.285), channel_id=1, replica_groups=mesh['member'=2,'section'=4,'atoms'=4] {'member'}, use_global_device_ids=true, to_apply=%region_10.11 | all-reduce | flops 256 | bytes 2048 | tf_op jit(solution)/shard_map/psum | solution.py:113
  163.6 0.7 fusion.80
  164.3 10.3 %pmax.7 = f32[2]{0:T(128)} all-reduce(f32[2]{0:T(128)S(1)} %get-tuple-element.283), channel_id=1, replica_groups=mesh['member'=2,'section'=4,'atoms'=4] {'atoms'}, use_global_device_ids=true, to_apply=%region_12.13 | all-reduce | flops 2 | bytes 16 | tf_op jit(solution)/shard_map/pmax | solution.py:115
  (121 shorter events, 18.8 us)
Async XLA Ops:
  0.6 47.2 %copy-start = (bf16[1,128,128]{2,1,0:T(8,128)(2,1)S(1)}, bf16[1,128,128]{2,1,0:T(8,128)(2,1)}, u32[]{:S(2)}) copy-start(bf16[1,128,128]{2,1,0:T(8,128)(2,1)} %param.15) | copy-start | bytes 98308
  49.8 10.9 %all-to-all-start = ((bf16[4,128,128]{2,1,0:T(8,128)(2,1)}), bf16[4,128,128]{2,1,0:T(8,128)(2,1)S(1)}, u32[]{:S(2)}, u32[]{:S(2)}) async-start(bf16[4,128,128]{2,1,0:T(8,128)(2,1)} %stack.48), calls=%async_computation | async-start | bytes 262144 | tf_op jit(solution)/shard_map/while/body/eval_jaxpr/all_to_all | solution.py:11
  64.1 11.7 %all-to-all-start.1 = ((bf16[4,128,128]{2,1,0:T(8,128)(2,1)}), bf16[4,128,128]{2,1,0:T(8,128)(2,1)S(1)}, u32[]{:S(2)}, u32[]{:S(2)}) async-start(bf16[4,128,128]{2,1,0:T(8,128)(2,1)} %stack.49), calls=%async_computation.1 | async-start | bytes 262144 | tf_op jit(solution)/shard_map/while/body/eval_jaxpr/all_to_all | solution.py:11
  79.3 9.5 %all-to-all-start.2 = ((bf16[4,128,128]{2,1,0:T(8,128)(2,1)}), bf16[4,128,128]{2,1,0:T(8,128)(2,1)S(1)}, u32[]{:S(2)}, u32[]{:S(2)}) async-start(bf16[4,128,128]{2,1,0:T(8,128)(2,1)} %stack.50), calls=%async_computation.2 | async-start | bytes 262144 | tf_op jit(solution)/shard_map/while/body/eval_jaxpr/all_to_all | solution.py:11
  92.2 9.2 %all-to-all-start.3 = ((bf16[4,128,128]{2,1,0:T(8,128)(2,1)}), bf16[4,128,128]{2,1,0:T(8,128)(2,1)S(1)}, u32[]{:S(2)}, u32[]{:S(2)}) async-start(bf16[4,128,128]{2,1,0:T(8,128)(2,1)} %stack.51), calls=%async_computation.3 | async-start | bytes 262144 | tf_op jit(solution)/shard_map/while/body/eval_jaxpr/all_to_all | solution.py:11
  105.4 10.8 %all-to-all-start = ((bf16[4,128,128]{2,1,0:T(8,128)(2,1)}), bf16[4,128,128]{2,1,0:T(8,128)(2,1)S(1)}, u32[]{:S(2)}, u32[]{:S(2)}) async-start(bf16[4,128,128]{2,1,0:T(8,128)(2,1)} %stack.48), calls=%async_computation | async-start | bytes 262144 | tf_op jit(solution)/shard_map/while/body/eval_jaxpr/all_to_all | solution.py:11
  119.7 10.9 %all-to-all-start.1 = ((bf16[4,128,128]{2,1,0:T(8,128)(2,1)}), bf16[4,128,128]{2,1,0:T(8,128)(2,1)S(1)}, u32[]{:S(2)}, u32[]{:S(2)}) async-start(bf16[4,128,128]{2,1,0:T(8,128)(2,1)} %stack.49), calls=%async_computation.1 | async-start | bytes 262144 | tf_op jit(solution)/shard_map/while/body/eval_jaxpr/all_to_all | solution.py:11
  134.1 9.2 %all-to-all-start.2 = ((bf16[4,128,128]{2,1,0:T(8,128)(2,1)}), bf16[4,128,128]{2,1,0:T(8,128)(2,1)S(1)}, u32[]{:S(2)}, u32[]{:S(2)}) async-start(bf16[4,128,128]{2,1,0:T(8,128)(2,1)} %stack.50), calls=%async_computation.2 | async-start | bytes 262144 | tf_op jit(solution)/shard_map/while/body/eval_jaxpr/all_to_all | solution.py:11
  146.8 9.2 %all-to-all-start.3 = ((bf16[4,128,128]{2,1,0:T(8,128)(2,1)}), bf16[4,128,128]{2,1,0:T(8,128)(2,1)S(1)}, u32[]{:S(2)}, u32[]{:S(2)}) async-start(bf16[4,128,128]{2,1,0:T(8,128)(2,1)} %stack.51), calls=%async_computation.3 | async-start | bytes 262144 | tf_op jit(solution)/shard_map/while/body/eval_jaxpr/all_to_all | solution.py:11
